TPU v7x, 32 devices: a whole 2x2x4 slice. The times are simulated.
32 devices in a mesh: dp: 16 (over z, y, core), mp: 2 (over x).
Axes of the slice: x: 2, y: 2, z: 4, core: 2. Of those that a mesh axis runs over, the one named last changes fastest.
Arguments:
- picture_tower_vectors: bfloat16 [3072, 1152], P('dp'), may hold values from -6 to 6
- caption_tower_vectors: bfloat16 [3072, 1152], P('dp', 'mp'), may hold values from -6 to 6
- picture_standardize_factor: float32 [1152], replicated, may hold values from 0.1 to 1.9
- picture_entry_matrix: bfloat16 [1152, 4304], P(None, 'mp'), may hold values from -0.1875 to 0.1875
- picture_exit_matrix: bfloat16 [4304, 1152], P('mp'), may hold values from -0.09375 to 0.09375
- caption_mapping_matrix: bfloat16 [1152, 1152], P('mp'), may hold values from -1 to 1
- energy_multiplier: float32 [], replicated, may hold values from 4 to 16
- energy_offset_term: float32 [], replicated, may hold values from -2 to -0.5
Outputs:
- grad_image: float32 [3072, 1152], P('dp', 'mp')
- grad_text: float32 [3072, 1152], P('dp', 'mp')
All inputs are finite; a program needn't handle non-finite values.
Results may differ from a plain program's by a relative error of at most 0.0046.
Values may be sent and summed in bfloat16 or wider, within the bound.
A program may use at most 64 MiB of HBM per device.

v0:
```python
import functools
import math

import jax
import jax.numpy as jnp
from jax import lax
from jax.experimental import pallas as pl
from jax.experimental.pallas import tpu as pltpu
from jax.sharding import PartitionSpec as P

F32 = jnp.float32
BF16 = jnp.bfloat16
MESH = pl.DeviceIdType.MESH
TILE = 512
ROOT = math.sqrt(2.0 / math.pi)
NT = (((1,), (1,)), ((), ()))


def dot(a, b):
    return jnp.dot(a, b, preferred_element_type=F32)


def dot_nt(a, b):
    return lax.dot_general(a, b, NT, preferred_element_type=F32)


def gelu_pair(x):
    square = x * x
    t = jnp.tanh(ROOT * (x + 0.044715 * (square * x)))
    half = 0.5 * (1.0 + t)
    slope = half + 0.5 * x * (1.0 - t * t) * (ROOT * (1.0 + 0.134145 * square))
    return x * half, slope


def norm_back(upstream, unit_rows, inverse):
    unit_float = unit_rows.astype(F32)
    along = jnp.sum(unit_float * upstream, axis=-1, keepdims=True)
    return inverse * (upstream - unit_float * along)


def body(
    n,
    heads,
    pic_hbm,
    cap_hbm,
    gain_ref,
    entry_hbm,
    exit_hbm,
    map_hbm,
    scale_ref,
    shift_ref,
    out_go,
    out_rest,
    out_text,
    pic,
    cap,
    entry,
    exit_,
    mapping,
    load_sem,
    normed,
    values,
    slope,
    weights,
    acc,
    own_f32,
    parts,
    lands,
    fulls,
    ring_text,
    ring_image,
    gains,
    centres,
    norm_own,
    norm_part,
    norm_land,
    sums_part,
    sums_land,
    part_send,
    part_recv,
    full_send,
    full_recv,
    norm_send,
    norm_recv,
    sums_send,
    sums_recv,
    ring_send,
    ring_recv,
):
    rows, width = pic.shape
    share = rows // heads
    hidden = exit_.shape[0]
    cols = width // heads
    me = lax.axis_index("dp")
    head = lax.axis_index("mp")
    length = n // 4

    def place(index):
        z = index // 4
        y = (index // 2) % 2
        return 2 * (z * (1 - y) + (2 * length - 1 - z) * y) + index % 2

    def device(position):
        position = (position + n) % n
        chip = position // 2
        y = chip // length
        z = chip * (1 - y) + (2 * length - 1 - chip) * y
        return (z * 2 + y) * 2 + position % 2

    pos = place(me)
    right = device(pos + 1)
    left = device(pos - 1)
    forward = n // 2
    backward = n - 1 - forward

    loads = []
    for at, (src, dst) in enumerate(
        (
            (cap_hbm, cap),
            (map_hbm, mapping),
            (pic_hbm, pic),
            (entry_hbm, entry),
            (exit_hbm, exit_),
        )
    ):
        copy = pltpu.make_async_copy(src, dst, load_sem.at[at])
        copy.start()
        loads.append(copy)

    barrier = pltpu.get_barrier_semaphore()
    for neighbour in (left, right):
        pl.semaphore_signal(barrier, inc=1, device_id={"dp": neighbour}, device_id_type=MESH)
    for o in range(1, heads):
        pl.semaphore_signal(
            barrier, inc=1, device_id={"mp": (head + o) % heads}, device_id_type=MESH
        )

    def ring_copy(which, buf, way, step):
        block = device(pos - step if way == 0 else pos + step)
        return pltpu.make_async_remote_copy(
            src_ref=buf.at[block],
            dst_ref=buf.at[block],
            send_sem=ring_send.at[which, way, step],
            recv_sem=ring_recv.at[which, way, step],
            device_id={"dp": right if way == 0 else left},
            device_id_type=MESH,
        )

    def ring_start(which, buf, step):
        if step < forward:
            ring_copy(which, buf, 0, step).start()
        if step < backward:
            ring_copy(which, buf, 1, step).start()

    def ring_next(which, buf, step):
        for way, count in ((0, forward), (1, backward)):
            if step < count:
                block = device(pos - step - 1 if way == 0 else pos + step + 1)
                pltpu.make_async_remote_copy(
                    src_ref=buf.at[block],
                    dst_ref=buf.at[block],
                    send_sem=ring_send.at[which, way, step],
                    recv_sem=ring_recv.at[which, way, step],
                    device_id={"dp": right if way == 0 else left},
                    device_id_type=MESH,
                ).wait_recv()
                if step + 1 < count:
                    ring_copy(which, buf, way, step + 1).start()

    def ring_end(which, buf):
        for way, count in ((0, forward), (1, backward)):
            for step in range(count):
                ring_copy(which, buf, way, step).wait_send()

    def exchange(src, dst, send, recv, spread, span=None):
        def part(ref, at):
            return ref.at[at] if span is None else ref.at[at, :, span]

        copies = []
        for o in range(1, heads):
            to = (head + o) % heads
            source = (head + heads - o) % heads
            sent = pltpu.make_async_remote_copy(
                src_ref=part(src, to if spread else head),
                dst_ref=part(dst, head),
                send_sem=send.at[o],
                recv_sem=recv.at[o],
                device_id={"mp": to},
                device_id_type=MESH,
            )
            got = pltpu.make_async_remote_copy(
                src_ref=part(dst, source),
                dst_ref=part(dst, source),
                send_sem=send.at[o],
                recv_sem=recv.at[o],
                device_id={"mp": to},
                device_id_type=MESH,
            )
            copies.append((sent, got))
        for sent, got in copies:
            sent.start()
        return copies

    def arrived(copies):
        for sent, got in copies:
            got.wait_recv()

    def finished(copies):
        for sent, got in copies:
            sent.wait_send()

    def scatter_start(which, product):
        copies = []
        for at, (first, size) in enumerate(pieces):
            columns = pl.ds(first, size)
            total = product(slice(first, first + size))
            for p in range(heads):
                piece = total[p * share : (p + 1) * share]
                own_f32[p, :, first : first + size] = piece
                parts[which, p, :, first : first + size] = piece.astype(BF16)
            copies += exchange(
                parts.at[which],
                lands.at[which],
                part_send.at[which, at],
                part_recv.at[which, at],
                True,
                columns,
            )
        return copies

    def scatter_sum(which, copies, mine):
        arrived(copies)
        for o in range(1, heads):
            mine = mine + lands[which, (head + heads - o) % heads].astype(F32)
        return mine

    def share_start(which, mine):
        fulls[which, head] = mine
        return exchange(
            fulls.at[which], fulls.at[which], full_send.at[which], full_recv.at[which], False
        )

    def full(which):
        return jnp.concatenate([fulls[which, p] for p in range(heads)], axis=0)

    pending = []
    pieces = [(first, min(TILE, width - first)) for first in range(0, width, TILE)]

    loads[0].wait()
    loads[1].wait()
    pl.semaphore_wait(barrier, 2 + heads - 1)
    text_copies = scatter_start(0, lambda span: dot(cap[...], mapping[:, span]))
    pending.append(text_copies)
    text_mine = own_f32[head]

    loads[2].wait()
    image_float = pic[...].astype(F32)
    mean_row = jnp.mean(image_float, axis=-1, keepdims=True)
    variance = jnp.mean((image_float - mean_row) ** 2, axis=-1, keepdims=True)
    inv_std = lax.rsqrt(variance + 1e-06)
    gain = gain_ref[...].reshape(1, width)
    centred = (image_float - mean_row) * inv_std
    normed[...] = (centred * gain).astype(BF16)
    for p in range(heads):
        gains[p] = gain[:, p * cols : (p + 1) * cols]
        centres[p] = centred[:, p * cols : (p + 1) * cols]

    text_out = scatter_sum(0, text_copies, text_mine)
    inv_text = lax.rsqrt(jnp.sum(text_out * text_out, axis=-1, keepdims=True) + 1e-06)
    unit_text = (text_out * inv_text).astype(BF16)
    ring_text[me] = unit_text
    ring_start(0, ring_text, 0)
    text_full = share_start(0, unit_text)
    pending.append(text_full)

    loads[3].wait()
    loads[4].wait()
    tiles = [(first, min(TILE, hidden - first)) for first in range(0, hidden, TILE)]
    text_steps = iter(range(forward))

    def advance(steps, which, buf, count):
        for _ in range(count):
            step = next(steps, None)
            if step is not None:
                ring_next(which, buf, step)

    for at, (first, size) in enumerate(tiles):
        span = slice(first, first + size)
        value, grad = gelu_pair(dot_nt(normed[...], entry[span, :]))
        slope[:, span] = grad
        values[:, span] = value.astype(BF16)
        if at % 2 == 1:
            advance(text_steps, 0, ring_text, 1)
    image_copies = scatter_start(1, lambda span: dot(values[...], exit_[:, span]))
    pending.append(image_copies)
    mine = own_f32[head] + pic[pl.ds(pl.multiple_of(head * share, 8), share), :].astype(F32)
    advance(text_steps, 0, ring_text, 2)
    image_out = scatter_sum(1, image_copies, mine)
    inv_image = lax.rsqrt(jnp.sum(image_out * image_out, axis=-1, keepdims=True) + 1e-06)
    unit_image = (image_out * inv_image).astype(BF16)
    ring_image[me] = unit_image
    image_full = share_start(1, unit_image)
    pending.append(image_full)
    ring_start(1, ring_image, 0)
    advance(text_steps, 0, ring_text, forward)
    ring_end(0, ring_text)
    arrived(image_full)
    arrived(text_full)

    scale = scale_ref[0, 0]
    shift = shift_ref[0, 0]
    group = 4 if share % 16 == 0 else 1

    def weigh(mine, block, g):
        energy = scale * dot_nt(mine, block) + shift
        shape = (rows, group * share)
        column = lax.broadcasted_iota(jnp.int32, shape, 1)
        ident = column + (g * (group * rows) + head * share)
        for j in range(1, group):
            ident = ident + jnp.where(column >= j * share, rows - share, 0)
        same = ident == lax.broadcasted_iota(jnp.int32, shape, 0) + me * rows
        weight = scale * jax.nn.sigmoid(jnp.where(same, -energy, energy))
        return jnp.where(same, -weight, weight).astype(BF16)

    def terms(rows_ref, buf):
        mine = full(rows_ref)
        if group > 1 and (group * share) % 128 == 0:
            for g in range(n // group):
                block = buf[g * group : (g + 1) * group].reshape(group * share, width)
                weights[:, g * group * share : (g + 1) * group * share] = weigh(mine, block, g)
            return lambda span: dot(
                weights[...], buf[:, :, span].reshape(n * share, span.stop - span.start)
            )
        acc[...] = jnp.zeros_like(acc)

        def one(g, carry):
            block = buf[g] if group == 1 else buf[pl.ds(g * group, group)].reshape(group * share, width)
            acc[...] += dot(weigh(full(rows_ref), block, g), block)
            return carry

        lax.fori_loop(0, n // group, one, 0)
        return lambda span: acc[:, span]

    image_steps = iter(range(forward))
    dir_copies = scatter_start(2, terms(1, ring_text))
    pending.append(dir_copies)
    dir_mine = own_f32[head]
    advance(image_steps, 1, ring_image, 4)
    image_dir = scatter_sum(2, dir_copies, dir_mine)
    grad_out = norm_back(image_dir, fulls[1, head], inv_image)
    grad_full = share_start(2, grad_out.astype(BF16))
    pending.append(grad_full)
    advance(image_steps, 1, ring_image, forward)
    ring_end(1, ring_image)

    dirs_copies = scatter_start(3, terms(0, ring_image))
    pending.append(dirs_copies)
    dirs_mine = own_f32[head]

    arrived(grad_full)
    for p in range(heads):
        out_go[p * share : (p + 1) * share] = fulls[2, p]
    grad_b = full(2)
    for at, (first, size) in enumerate(tiles):
        span = slice(first, first + size)
        values[:, span] = (dot_nt(grad_b, exit_[span, :]) * slope[:, span]).astype(BF16)
    total = dot(values[...], entry[...])
    for p in range(heads):
        piece = total[:, p * cols : (p + 1) * cols]
        norm_own[p] = piece
        norm_part[p] = piece.astype(BF16)
    norm_copies = exchange(norm_part, norm_land, norm_send, norm_recv, True)
    scaled = total * gain_ref[...].reshape(1, width)
    one_sum = jnp.sum(scaled, axis=-1, keepdims=True)
    centred = (pic[...].astype(F32) - mean_row) * inv_std
    two_sum = jnp.sum(scaled * centred, axis=-1, keepdims=True)
    lane = lax.broadcasted_iota(jnp.int32, (rows, 128), 1)
    sums_part[head] = jnp.where(lane == 0, one_sum, two_sum)
    sums_copies = exchange(sums_part, sums_land, sums_send, sums_recv, False)
    pending.append(norm_copies)
    pending.append(sums_copies)

    text_dir = scatter_sum(3, dirs_copies, dirs_mine)
    grad_text_out = norm_back(text_dir, fulls[0, head], inv_text).astype(BF16)
    last_full = share_start(3, grad_text_out)
    pending.append(last_full)

    arrived(norm_copies)
    arrived(sums_copies)
    grad_normed = norm_own[head]
    sums = sums_part[head]
    for o in range(1, heads):
        source = (head + heads - o) % heads
        grad_normed = grad_normed + norm_land[source].astype(F32)
        sums = sums + sums_land[source]
    mean_one = sums[:, 0:1] * (1.0 / width)
    mean_two = sums[:, 1:2] * (1.0 / width)
    centred = centres[head]
    scaled = grad_normed * gains[head]
    out_rest[...] = inv_std * (scaled - mean_one - centred * mean_two)

    arrived(last_full)
    out_text[...] = dot_nt(full(3), mapping[...])
    for copies in pending:
        finished(copies)


def per_device(pic, cap, gain, entry, exit_, mapping, scale, shift):
    rows, width = pic.shape
    n = lax.axis_size("dp")
    heads = lax.axis_size("mp")
    cols = cap.shape[1]
    share = rows // heads
    hidden = entry.shape[1]
    flipped = entry.T
    anywhere = pl.BlockSpec(memory_space=pl.ANY)
    vmem = pl.BlockSpec(memory_space=pltpu.VMEM)
    smem = pl.BlockSpec(memory_space=pltpu.SMEM)
    dma = pltpu.SemaphoreType.DMA
    go, rest, text = pl.pallas_call(
        functools.partial(body, n, heads),
        out_shape=(
            jax.ShapeDtypeStruct((rows, width), BF16),
            jax.ShapeDtypeStruct((rows, cols), F32),
            jax.ShapeDtypeStruct((rows, mapping.shape[0]), F32),
        ),
        in_specs=[anywhere, anywhere, vmem, anywhere, anywhere, anywhere, smem, smem],
        out_specs=(vmem, vmem, vmem),
        scratch_shapes=[
            pltpu.VMEM(pic.shape, BF16),
            pltpu.VMEM(cap.shape, BF16),
            pltpu.VMEM(flipped.shape, BF16),
            pltpu.VMEM(exit_.shape, BF16),
            pltpu.VMEM(mapping.shape, BF16),
            dma((5,)),
            pltpu.VMEM((rows, width), BF16),
            pltpu.VMEM((rows, hidden), BF16),
            pltpu.VMEM((rows, hidden), F32),
            pltpu.VMEM((rows, n * share), BF16),
            pltpu.VMEM((rows, width), F32),
            pltpu.VMEM((heads, share, width), F32),
            pltpu.VMEM((4, heads, share, width), BF16),
            pltpu.VMEM((4, heads, share, width), BF16),
            pltpu.VMEM((4, heads, share, width), BF16),
            pltpu.VMEM((n, share, width), BF16),
            pltpu.VMEM((n, share, width), BF16),
            pltpu.VMEM((heads, 1, cols), F32),
            pltpu.VMEM((heads, rows, cols), F32),
            pltpu.VMEM((heads, rows, cols), F32),
            pltpu.VMEM((heads, rows, cols), BF16),
            pltpu.VMEM((heads, rows, cols), BF16),
            pltpu.VMEM((heads, rows, 128), F32),
            pltpu.VMEM((heads, rows, 128), F32),
            dma((4, pl.cdiv(width, TILE), heads)),
            dma((4, pl.cdiv(width, TILE), heads)),
            dma((4, heads)),
            dma((4, heads)),
            dma((heads,)),
            dma((heads,)),
            dma((heads,)),
            dma((heads,)),
            dma((2, 2, n // 2)),
            dma((2, 2, n // 2)),
        ],
        compiler_params=pltpu.CompilerParams(
            collective_id=0, has_side_effects=True, vmem_limit_bytes=60 * 2**20
        ),
        name="contrastive",
    )(
        pic,
        cap,
        gain,
        flipped,
        exit_,
        mapping,
        scale.reshape(1, 1),
        shift.reshape(1, 1),
    )
    first = lax.axis_index("mp") * cols
    grad_image = lax.dynamic_slice_in_dim(go, first, cols, 1).astype(F32) + rest
    return grad_image, text


def solution(mesh):
    in_specs = (
        P("dp", None),
        P("dp", "mp"),
        P(),
        P(None, "mp"),
        P("mp", None),
        P("mp", None),
        P(),
        P(),
    )
    out_specs = (P("dp", "mp"), P("dp", "mp"))
    return jax.shard_map(
        per_device, mesh=mesh, in_specs=in_specs, out_specs=out_specs, check_vma=False
    )
```

profile of v0, /device:TPU:0, one launch (start us, length us, event | category | flops | bytes accessed | tf_op | source)
XLA Modules:
  0.0 93.1 jit_solution(13613528140270850321)
XLA Ops:
  1.9 87.3 %contrastive.1 = (bf16[192,1152]{1,0:T(8,128)(2,1)}, f32[192,576]{1,0:T(8,128)}, f32[192,576]{1,0:T(8,128)}) custom-call(bf16[192,1152]{1,0:T(8,128)(2,1)} %pic_hbm.1, bf16[192,576]{1,0:T(8,128)(2,1)} %cap_hbm.1, f32[1152]{0:T(1024)} %gain_ref.1, bf16[2152,1152]{1,0:T(8,128)(2,1)} %bitcast.5, bf16[2152,1152]{1,0:T(8,128)(2,1)} %exit_hbm.1, ...), custom_call_target="tpu_custom_call" | custom-call | tf_op jit(solution)/shard_map/contrastive/pallas_call | solution.py:420
  89.2 2.0 %convert_add_fusion = f32[192,576]{1,0:T(8,128)} fusion(f32[192,576]{1,0:T(8,128)} %get-tuple-element.6, bf16[192,1152]{1,0:T(8,128)(2,1)} %get-tuple-element.5, s32[]{:T(128)S(6)} %select_n.3), kind=kLoop, calls=%fused_computation | loop fusion | flops 221184 | bytes 1105924 | tf_op jit(solution)/shard_map/add | solution.py:480
  91.2 1.8 %copy.13 = f32[192,576]{1,0:T(8,128)} copy(f32[192,576]{1,0:T(8,128)} %get-tuple-element.11) | data formatting | bytes 884736
where the time goes:
time: 93.3 us; the launch traced here: 93.1 us
  Pallas kernels  87.3 us (94%)
  other arithmetic  2.03 us (2%)
  between operations  1.93 us (2%)
  local copies, waits for them, and re-layouts  1.84 us (2%)
    pallas_call x1, Pallas kernels, per_device(): pl.pallas_call(functools.partial(body, n, heads), out_shape=(jax.ShapeDty...  87.3 us
    add x1, other arithmetic, per_device(): grad_image = lax.dynamic_slice_in_dim(go, first, cols, 1).astype(F32) + rest  2.03 us

commit v1 on v0

--- a/solution.py
+++ b/solution.py
@@ -14,6 +14,7 @@
 TILE = 512
 ROOT = math.sqrt(2.0 / math.pi)
 NT = (((1,), (1,)), ((), ()))
+TN = (((0,), (0,)), ((), ()))
 
 
 def dot(a, b):
@@ -481,6 +482,401 @@
     return grad_image, text
 
 
+def flipped_bit(index, bit):
+    return index + bit * (1 - 2 * ((index // bit) % 2))
+
+
+def dot_tn(a, b):
+    return lax.dot_general(a, b, TN, preferred_element_type=F32)
+
+
+def split_three(x):
+    high = x.astype(BF16)
+    rest = x - high.astype(F32)
+    middle = rest.astype(BF16)
+    return high, middle, (rest - middle.astype(F32)).astype(BF16)
+
+
+def square_body(
+    pic_hbm,
+    cap_hbm,
+    gain_ref,
+    entry_hbm,
+    exit_hbm,
+    map_hbm,
+    scale_ref,
+    shift_ref,
+    out_image,
+    out_text,
+    pic,
+    cap,
+    entry,
+    exit_,
+    mapping,
+    load_sem,
+    normed,
+    centred_ref,
+    values,
+    slope,
+    t_own,
+    t_part,
+    t_land,
+    i_own,
+    i_part,
+    i_land,
+    tbuf,
+    ibuf,
+    weights,
+    d_own,
+    d_part,
+    d_land,
+    g_part,
+    g_land,
+    s_own,
+    c_part,
+    c_land,
+    y_part,
+    y_land,
+    h_part,
+    h_land,
+    gt_part,
+    gt_land,
+    n_part,
+    n_land,
+    send_sem,
+    recv_sem,
+):
+    rows, width = pic.shape
+    share = rows // 2
+    hidden = exit_.shape[0]
+    cols = width // 2
+    me = lax.axis_index("dp")
+    head = lax.axis_index("mp")
+    other = 1 - head
+    by_core = {"dp": flipped_bit(me, 1)}
+    by_y = {"dp": flipped_bit(me, 2)}
+    by_low = {"dp": flipped_bit(me, 4)}
+    by_high = {"dp": flipped_bit(me, 8)}
+    by_x = {"mp": other}
+    by_both = {"dp": flipped_bit(me, 4), "mp": other}
+    own_rows = pl.ds(pl.multiple_of(head * share, 16), share)
+    other_rows = pl.ds(pl.multiple_of(other * share, 16), share)
+    top = pl.ds(0, share)
+    bottom = pl.ds(share, share)
+    tiles = [(first, min(TILE, hidden - first)) for first in range(0, hidden, TILE)]
+    piece = width // 3 if width % 384 == 0 else width
+    spans = [slice(first, first + piece) for first in range(0, width, piece)]
+
+    load_count = 0
+
+    def load(src, dst):
+        nonlocal load_count
+        copy = pltpu.make_async_copy(src, dst, load_sem.at[load_count])
+        load_count += 1
+        copy.start()
+        return copy
+
+    cap_loads = [
+        load(cap_hbm.at[own_rows], cap.at[top]),
+        load(cap_hbm.at[other_rows], cap.at[bottom]),
+        load(map_hbm, mapping),
+    ]
+    pic_loads = [
+        load(pic_hbm.at[own_rows], pic.at[top]),
+        load(pic_hbm.at[other_rows], pic.at[bottom]),
+    ]
+    entry_loads = [
+        load(entry_hbm.at[pl.ds(first, size)], entry.at[pl.ds(first, size)]) for first, size in tiles
+    ]
+    exit_loads = [
+        load(exit_hbm.at[pl.ds(first, size)], exit_.at[pl.ds(first, size)]) for first, size in tiles
+    ]
+
+    barrier = pltpu.get_barrier_semaphore()
+    partners = (by_x, by_y, by_high, by_low, by_both, by_core)
+    for partner in partners:
+        pl.semaphore_signal(barrier, inc=1, device_id=partner, device_id_type=MESH)
+
+    pending = []
+
+    def push(src, dst, partner):
+        at = len(pending)
+        copy = pltpu.make_async_remote_copy(
+            src_ref=src,
+            dst_ref=dst,
+            send_sem=send_sem.at[at],
+            recv_sem=recv_sem.at[at],
+            device_id=partner,
+            device_id_type=MESH,
+        )
+        copy.start()
+        pending.append(copy)
+        return copy
+
+    def arrived(copies):
+        for copy in copies:
+            copy.wait_recv()
+
+    def slot(ref, at, span=slice(None)):
+        return ref.at[pl.ds(at * share, share), span]
+
+    for copy in cap_loads:
+        copy.wait()
+    text_partials = []
+    for at, span in enumerate(spans):
+        total = dot(cap[...], mapping[:, span])
+        t_own[:, span] = total[:share]
+        t_part[:, span] = total[share:].astype(BF16)
+        if at == 0:
+            pl.semaphore_wait(barrier, len(partners))
+        text_partials.append(push(t_part.at[:, span], t_land.at[:, span], by_x))
+
+    for copy in pic_loads:
+        copy.wait()
+    image_float = pic[...].astype(F32)
+    mean_row = jnp.mean(image_float, axis=-1, keepdims=True)
+    variance = jnp.mean((image_float - mean_row) ** 2, axis=-1, keepdims=True)
+    inv_std = lax.rsqrt(variance + 1e-06)
+    gain = gain_ref[...].reshape(1, width)
+    centred = (image_float - mean_row) * inv_std
+    centred_ref[...] = centred
+    normed[...] = (centred * gain).astype(BF16)
+
+    for (first, size), copy in zip(tiles, entry_loads):
+        copy.wait()
+        span = slice(first, first + size)
+        value, grad = gelu_pair(dot_nt(normed[...], entry[span, :]))
+        slope[:, span] = grad
+        values[:, span] = value.astype(BF16)
+    for copy in exit_loads:
+        copy.wait()
+    image_partials = []
+    for span in spans:
+        total = dot(values[...], exit_[:, span])
+        i_own[:, span] = total[:share] + pic[:share, span].astype(F32)
+        i_part[:, span] = total[share:].astype(BF16)
+        image_partials.append(push(i_part.at[:, span], i_land.at[:, span], by_x))
+
+    arrived(text_partials)
+    text_out = t_own[...] + t_land[...].astype(F32)
+    inv_text = lax.rsqrt(jnp.sum(text_out * text_out, axis=-1, keepdims=True) + 1e-06)
+    tbuf[:share] = (text_out * inv_text).astype(BF16)
+    high_copies = [push(slot(tbuf, 0, span), slot(tbuf, 4, span), by_high) for span in spans]
+    y_copy = push(slot(tbuf, 0), slot(tbuf, 2), by_y)
+    core_copies = [push(slot(tbuf, 0), slot(tbuf, 1), by_core)]
+
+    arrived(image_partials)
+    image_out = i_own[...] + i_land[...].astype(F32)
+    inv_image = lax.rsqrt(jnp.sum(image_out * image_out, axis=-1, keepdims=True) + 1e-06)
+    ibuf[:share] = (image_out * inv_image).astype(BF16)
+    image_copies = [
+        push(slot(ibuf, 0), slot(ibuf, 3), by_both),
+        push(slot(ibuf, 0), slot(ibuf, 1), by_x),
+        push(slot(ibuf, 0), slot(ibuf, 2), by_low),
+    ]
+
+    diagonal_copies = []
+    for copy, span in zip(high_copies, spans):
+        copy.wait_recv()
+        diagonal_copies.append(push(slot(tbuf, 4, span), slot(tbuf, 6, span), by_y))
+        core_copies.append(push(slot(tbuf, 4, span), slot(tbuf, 5, span), by_core))
+    y_copy.wait_recv()
+    core_copies.append(push(slot(tbuf, 2), slot(tbuf, 3), by_core))
+    for copy, span in zip(diagonal_copies, spans):
+        copy.wait_recv()
+        core_copies.append(push(slot(tbuf, 6, span), slot(tbuf, 7, span), by_core))
+    arrived(core_copies)
+    arrived(image_copies)
+
+    scale = scale_ref[0, 0]
+    shift = shift_ref[0, 0]
+    texts = 8 * share
+    group = texts // 3 if texts % 384 == 0 else texts
+    for first in range(0, texts, group):
+        energy = scale * dot_nt(ibuf[...], tbuf[first : first + group, :]) + shift
+        row = lax.broadcasted_iota(jnp.int32, energy.shape, 0)
+        column = lax.broadcasted_iota(jnp.int32, energy.shape, 1) + first
+        same = jnp.logical_and(row == column, row < share)
+        weight = scale * jax.nn.sigmoid(jnp.where(same, -energy, energy))
+        weights[:, first : first + group] = jnp.where(same, -weight, weight).astype(BF16)
+
+    dir_copies = []
+    for span in spans:
+        total = dot(weights[...], tbuf[:, span])
+        d_own[:, span] = total[:share]
+        d_part[:, span] = total[share:].astype(BF16)
+        for at, partner in ((2, by_both), (0, by_x), (1, by_low)):
+            dir_copies.append(push(slot(d_part, at, span), slot(d_land, at, span), partner))
+
+    core_copies = []
+    for span in spans:
+        total = dot_tn(weights[...], ibuf[:, span])
+        for at in range(4):
+            first = 2 * at * share
+            s_own[at, :, span] = total[first : first + share]
+            c_part[at * share : (at + 1) * share, span] = total[
+                first + share : first + 2 * share
+            ].astype(BF16)
+        core_copies.append(push(c_part.at[:, span], c_land.at[:, span], by_core))
+    diagonal_copies = []
+    for copy, span in zip(core_copies, spans):
+        copy.wait_recv()
+        for at in range(4):
+            total = s_own[at, :, span] + c_land[at * share : (at + 1) * share, span].astype(F32)
+            if at % 2:
+                first = (at // 2) * share
+                y_part[first : first + share, span] = total.astype(BF16)
+            else:
+                s_own[at, :, span] = total
+        diagonal_copies.append(push(slot(y_part, 1, span), slot(y_land, 1, span), by_y))
+    y_copies = [push(slot(y_part, 0, span), slot(y_land, 0, span), by_y) for span in spans]
+    high_copies = []
+    for copy, span in zip(diagonal_copies, spans):
+        copy.wait_recv()
+        h_part[:, span] = (s_own[2, :, span] + y_land[share:, span].astype(F32)).astype(BF16)
+        high_copies.append(push(h_part.at[:, span], h_land.at[:, span], by_high))
+
+    arrived(dir_copies)
+    image_dir = d_own[...]
+    for at in range(3):
+        image_dir = image_dir + d_land[at * share : (at + 1) * share, :].astype(F32)
+    grad_out = norm_back(image_dir, ibuf[:share], inv_image)
+    g_part[...] = grad_out.astype(BF16)
+    grad_copy = push(g_part, g_land, by_x)
+
+    grad_copy.wait_recv()
+    grad_b = jnp.concatenate([g_part[...], g_land[...]], axis=0)
+    for first, size in tiles:
+        span = slice(first, first + size)
+        values[:, span] = (dot_nt(grad_b, exit_[span, :]) * slope[:, span]).astype(BF16)
+    total = dot(values[...], entry[...])
+    mine_first = head == 0
+    lower = total[:, :cols]
+    upper = total[:, cols:]
+    theirs = jnp.where(mine_first, upper, lower).astype(BF16)
+    n_part[:share, :cols] = theirs[share:]
+    n_part[share:, :cols] = theirs[:share]
+    grad_normed = jnp.where(mine_first, lower, upper)
+    scaled = total * gain_ref[...].reshape(1, width)
+    centred = centred_ref[...]
+    one_sum = jnp.sum(scaled, axis=-1, keepdims=True)
+    two_sum = jnp.sum(scaled * centred, axis=-1, keepdims=True)
+    lane = lax.broadcasted_iota(jnp.int32, (rows, n_part.shape[1] - cols), 1)
+    packed = jnp.zeros(lane.shape, F32)
+    for at, term in enumerate(split_three(one_sum) + split_three(two_sum)):
+        packed = jnp.where(lane == at, term.astype(F32), packed)
+    n_part[:share, cols:] = packed[share:].astype(BF16)
+    n_part[share:, cols:] = packed[:share].astype(BF16)
+    norm_copy = push(n_part, n_land, by_x)
+
+    arrived(y_copies)
+    arrived(high_copies)
+    text_dir = s_own[0] + y_land[:share, :].astype(F32) + h_land[...].astype(F32)
+    gt_part[...] = norm_back(text_dir, tbuf[:share], inv_text).astype(BF16)
+    text_copy = push(gt_part, gt_land, by_x)
+
+    norm_copy.wait_recv()
+    gains = gain_ref[...].reshape(1, width)
+    gains = jnp.where(mine_first, gains[:, :cols], gains[:, cols:])
+    centred = jnp.where(mine_first, centred[:, :cols], centred[:, cols:])
+    grad_float = grad_b.astype(F32)
+    grad_float = jnp.where(mine_first, grad_float[:, :cols], grad_float[:, cols:])
+    grad_normed = grad_normed + n_land[:, :cols].astype(F32)
+    sums = n_land[:, cols:].astype(F32)
+    mean_one = (one_sum + (sums[:, 0:1] + sums[:, 1:2] + sums[:, 2:3])) * (1.0 / width)
+    mean_two = (two_sum + (sums[:, 3:4] + sums[:, 4:5] + sums[:, 5:6])) * (1.0 / width)
+    result = grad_float + inv_std * (grad_normed * gains - mean_one - centred * mean_two)
+    out_image[own_rows, :] = result[:share]
+    out_image[other_rows, :] = result[share:]
+
+    text_copy.wait_recv()
+    result = dot_nt(jnp.concatenate([gt_part[...], gt_land[...]], axis=0), mapping[...])
+    out_text[own_rows, :] = result[:share]
+    out_text[other_rows, :] = result[share:]
+    for copy in pending:
+        copy.wait_send()
+
+
+def square_device(pic, cap, gain, entry, exit_, mapping, scale, shift):
+    rows, width = pic.shape
+    cols = cap.shape[1]
+    share = rows // 2
+    hidden = entry.shape[1]
+    flipped = entry.T
+    anywhere = pl.BlockSpec(memory_space=pl.ANY)
+    vmem = pl.BlockSpec(memory_space=pltpu.VMEM)
+    smem = pl.BlockSpec(memory_space=pltpu.SMEM)
+    dma = pltpu.SemaphoreType.DMA
+
+    def blocks(count, dtype=BF16):
+        return pltpu.VMEM((count * share, width), dtype)
+
+    loads = 5 + 2 * pl.cdiv(hidden, TILE)
+    copies = 64
+    extended = 128 * (cols // 128 + 1)
+    return pl.pallas_call(
+        square_body,
+        out_shape=(
+            jax.ShapeDtypeStruct((rows, cols), F32),
+            jax.ShapeDtypeStruct((rows, mapping.shape[0]), F32),
+        ),
+        in_specs=[anywhere, anywhere, vmem, anywhere, anywhere, anywhere, smem, smem],
+        out_specs=(vmem, vmem),
+        scratch_shapes=[
+            pltpu.VMEM(pic.shape, BF16),
+            pltpu.VMEM(cap.shape, BF16),
+            pltpu.VMEM(flipped.shape, BF16),
+            pltpu.VMEM(exit_.shape, BF16),
+            pltpu.VMEM(mapping.shape, BF16),
+            dma((loads,)),
+            pltpu.VMEM((rows, width), BF16),
+            pltpu.VMEM((rows, width), F32),
+            pltpu.VMEM((rows, hidden), BF16),
+            pltpu.VMEM((rows, hidden), F32),
+            blocks(1, F32),
+            blocks(1),
+            blocks(1),
+            blocks(1, F32),
+            blocks(1),
+            blocks(1),
+            blocks(8),
+            blocks(4),
+            pltpu.VMEM((4 * share, 8 * share), BF16),
+            blocks(1, F32),
+            blocks(3),
+            blocks(3),
+            blocks(1),
+            blocks(1),
+            pltpu.VMEM((4, share, width), F32),
+            blocks(4),
+            blocks(4),
+            blocks(2),
+            blocks(2),
+            blocks(1),
+            blocks(1),
+            blocks(1),
+            blocks(1),
+            pltpu.VMEM((rows, extended), BF16),
+            pltpu.VMEM((rows, extended), BF16),
+            dma((copies,)),
+            dma((copies,)),
+        ],
+        compiler_params=pltpu.CompilerParams(
+            collective_id=0, has_side_effects=True, vmem_limit_bytes=60 * 2**20
+        ),
+        name="contrastive_square",
+    )(
+        pic,
+        cap,
+        gain,
+        flipped,
+        exit_,
+        mapping,
+        scale.reshape(1, 1),
+        shift.reshape(1, 1),
+    )
+
+
 def solution(mesh):
     in_specs = (
         P("dp", None),
@@ -493,6 +889,7 @@
         P(),
     )
     out_specs = (P("dp", "mp"), P("dp", "mp"))
+    square = mesh.shape["mp"] == 2 and mesh.shape["dp"] == 16
     return jax.shard_map(
-        per_device, mesh=mesh, in_specs=in_specs, out_specs=out_specs, check_vma=False
+        square_device if square else per_device, mesh=mesh, in_specs=in_specs, out_specs=out_specs, check_vma=False
     )

time: 93.3 us -> 74.9 us (0.80)
  Pallas kernels: 87.3 us -> 69.1 us
  other arithmetic: 2.03 us -> 0 us
  local copies, waits for them, and re-layouts: 1.84 us -> 3.68 us
    pallas_call x1, Pallas kernels: 87.3 us -> 69.1 us  [square_device(): pl.pallas_call(square_body, out_shape=(jax.ShapeDtypeStruct((rows, cols),...]
    add x1 -> x0, other arithmetic: 2.03 us -> none  [per_device(): grad_image = lax.dynamic_slice_in_dim(go, first, cols, 1).astype(F32) + rest]
    unnamed x1 -> x2, local copies, waits for them, and re-layouts: 1.84 us -> 3.68 us
where the time goes in v1:
time: 74.9 us; the launch traced here: 74.7 us
  Pallas kernels  69.1 us (92%)
  local copies, waits for them, and re-layouts  3.68 us (5%)
  between operations  1.93 us (3%)
    pallas_call x1, Pallas kernels, square_device(): pl.pallas_call(square_body, out_shape=(jax.ShapeDtypeStruct((rows, cols),...  69.1 us
    unnamed x2, local copies, waits for them, and re-layouts  3.68 us

profile of v1, /device:TPU:0, one launch (start us, length us, event | category | flops | bytes accessed | tf_op | source)
XLA Modules:
  0.0 74.7 jit_solution(4340226812503939605)
XLA Ops:
  1.9 69.1 %contrastive_square.1 = (f32[192,576]{1,0:T(8,128)}, f32[192,576]{1,0:T(8,128)}) custom-call(bf16[192,1152]{1,0:T(8,128)(2,1)} %pic_hbm.1, bf16[192,576]{1,0:T(8,128)(2,1)} %cap_hbm.1, f32[1152]{0:T(1024)} %gain_ref.1, bf16[2152,1152]{1,0:T(8,128)(2,1)} %bitcast.5, bf16[2152,1152]{1,0:T(8,128)(2,1)} %exit_hbm.1, bf16[576,1152]{1,0:T(8,128)(2,1)} %map_hbm.1, ...), custom_call_target="tpu_custom_call" | custom-call | tf_op jit(solution)/shard_map/contrastive_square/pallas_call | solution.py:817
  71.0 1.8 %copy.14 = f32[192,576]{1,0:T(8,128)} copy(f32[192,576]{1,0:T(8,128)} %get-tuple-element.4) | data formatting | bytes 884736
  72.8 1.8 %copy.15 = f32[192,576]{1,0:T(8,128)} copy(f32[192,576]{1,0:T(8,128)} %get-tuple-element.5) | data formatting | bytes 884736

commit v2 on v1

--- a/solution.py
+++ b/solution.py
@@ -500,7 +500,7 @@
 def square_body(
     pic_hbm,
     cap_hbm,
-    gain_ref,
+    gain_hbm,
     entry_hbm,
     exit_hbm,
     map_hbm,
@@ -510,6 +510,7 @@
     out_text,
     pic,
     cap,
+    gain_ref,
     entry,
     exit_,
     mapping,
@@ -528,7 +529,9 @@
     ibuf,
     weights,
     d_own,
+    d_near,
     d_part,
+    d_through,
     d_land,
     g_part,
     g_land,
@@ -558,14 +561,24 @@
     by_low = {"dp": flipped_bit(me, 4)}
     by_high = {"dp": flipped_bit(me, 8)}
     by_x = {"mp": other}
-    by_both = {"dp": flipped_bit(me, 4), "mp": other}
     own_rows = pl.ds(pl.multiple_of(head * share, 16), share)
     other_rows = pl.ds(pl.multiple_of(other * share, 16), share)
-    top = pl.ds(0, share)
-    bottom = pl.ds(share, share)
     tiles = [(first, min(TILE, hidden - first)) for first in range(0, hidden, TILE)]
-    piece = width // 3 if width % 384 == 0 else width
-    spans = [slice(first, first + piece) for first in range(0, width, piece)]
+    chunk = share // 2 if share % 32 == 0 else share
+    chunks = range(share // chunk)
+    spans = [slice(first, min(first + TILE, width)) for first in range(0, width, TILE)]
+
+    def block(ref, at):
+        return ref.at[pl.ds(at * share, share)]
+
+    def part(ref, at, k):
+        return ref.at[pl.ds(at * share + k * chunk, chunk)]
+
+    def of(at):
+        return slice(at * share, (at + 1) * share)
+
+    def lines(at, k):
+        return slice(at * share + k * chunk, at * share + (k + 1) * chunk)
 
     load_count = 0
 
@@ -577,13 +590,14 @@
         return copy
 
     cap_loads = [
-        load(cap_hbm.at[own_rows], cap.at[top]),
-        load(cap_hbm.at[other_rows], cap.at[bottom]),
+        load(cap_hbm.at[other_rows], block(cap, 1)),
         load(map_hbm, mapping),
+        load(cap_hbm.at[own_rows], block(cap, 0)),
     ]
     pic_loads = [
-        load(pic_hbm.at[own_rows], pic.at[top]),
-        load(pic_hbm.at[other_rows], pic.at[bottom]),
+        load(pic_hbm.at[own_rows], block(pic, 0)),
+        load(pic_hbm.at[other_rows], block(pic, 1)),
+        load(gain_hbm, gain_ref),
     ]
     entry_loads = [
         load(entry_hbm.at[pl.ds(first, size)], entry.at[pl.ds(first, size)]) for first, size in tiles
@@ -593,7 +607,7 @@
     ]
 
     barrier = pltpu.get_barrier_semaphore()
-    partners = (by_x, by_y, by_high, by_low, by_both, by_core)
+    partners = (by_x, by_y, by_high, by_low, by_core)
     for partner in partners:
         pl.semaphore_signal(barrier, inc=1, device_id=partner, device_id_type=MESH)
 
@@ -617,19 +631,12 @@
         for copy in copies:
             copy.wait_recv()
 
-    def slot(ref, at, span=slice(None)):
-        return ref.at[pl.ds(at * share, share), span]
-
     for copy in cap_loads:
         copy.wait()
-    text_partials = []
-    for at, span in enumerate(spans):
-        total = dot(cap[...], mapping[:, span])
-        t_own[:, span] = total[:share]
-        t_part[:, span] = total[share:].astype(BF16)
-        if at == 0:
-            pl.semaphore_wait(barrier, len(partners))
-        text_partials.append(push(t_part.at[:, span], t_land.at[:, span], by_x))
+    t_part[...] = dot(cap[share:], mapping[...]).astype(BF16)
+    pl.semaphore_wait(barrier, len(partners))
+    text_partials = [push(part(t_part, 0, k), part(t_land, 0, k), by_x) for k in chunks]
+    t_own[...] = dot(cap[:share], mapping[...])
 
     for copy in pic_loads:
         copy.wait()
@@ -648,45 +655,67 @@
         value, grad = gelu_pair(dot_nt(normed[...], entry[span, :]))
         slope[:, span] = grad
         values[:, span] = value.astype(BF16)
+
+    def unit_rows(own, land, k, dst):
+        total = own[lines(0, k)] + land[lines(0, k)].astype(F32)
+        inverse = lax.rsqrt(jnp.sum(total * total, axis=-1, keepdims=True) + 1e-06)
+        dst[lines(0, k)] = (total * inverse).astype(BF16)
+        return inverse
+
+    inv_text = []
+    high_copies = []
+    y_copies = []
+    core_copies = []
+
+    def text_chunk(k):
+        text_partials[k].wait_recv()
+        inv_text.append(unit_rows(t_own, t_land, k, tbuf))
+        high_copies.append(push(part(tbuf, 0, k), part(tbuf, 2, k), by_high))
+        y_copies.append(push(part(tbuf, 0, k), part(tbuf, 1, k), by_y))
+        core_copies.append(push(part(tbuf, 0, k), part(tbuf, 4, k), by_core))
+
+    text_chunk(0)
     for copy in exit_loads:
         copy.wait()
-    image_partials = []
     for span in spans:
-        total = dot(values[...], exit_[:, span])
-        i_own[:, span] = total[:share] + pic[:share, span].astype(F32)
-        i_part[:, span] = total[share:].astype(BF16)
-        image_partials.append(push(i_part.at[:, span], i_land.at[:, span], by_x))
-
-    arrived(text_partials)
-    text_out = t_own[...] + t_land[...].astype(F32)
-    inv_text = lax.rsqrt(jnp.sum(text_out * text_out, axis=-1, keepdims=True) + 1e-06)
-    tbuf[:share] = (text_out * inv_text).astype(BF16)
-    high_copies = [push(slot(tbuf, 0, span), slot(tbuf, 4, span), by_high) for span in spans]
-    y_copy = push(slot(tbuf, 0), slot(tbuf, 2), by_y)
-    core_copies = [push(slot(tbuf, 0), slot(tbuf, 1), by_core)]
-
-    arrived(image_partials)
-    image_out = i_own[...] + i_land[...].astype(F32)
-    inv_image = lax.rsqrt(jnp.sum(image_out * image_out, axis=-1, keepdims=True) + 1e-06)
-    ibuf[:share] = (image_out * inv_image).astype(BF16)
-    image_copies = [
-        push(slot(ibuf, 0), slot(ibuf, 3), by_both),
-        push(slot(ibuf, 0), slot(ibuf, 1), by_x),
-        push(slot(ibuf, 0), slot(ibuf, 2), by_low),
-    ]
-
+        i_part[:, span] = dot(values[share:], exit_[:, span]).astype(BF16)
+    image_partials = [push(part(i_part, 0, k), part(i_land, 0, k), by_x) for k in chunks]
+    for k in chunks[1:]:
+        text_chunk(k)
+    for span in spans:
+        i_own[:, span] = dot(values[:share], exit_[:, span]) + pic[:share, span].astype(F32)
+
+    inv_image = []
+    x_copies = []
+    low_copies = []
+    for k in chunks:
+        image_partials[k].wait_recv()
+        inv_image.append(unit_rows(i_own, i_land, k, ibuf))
+        x_copies.append(push(part(ibuf, 0, k), part(ibuf, 1, k), by_x))
+        low_copies.append(push(part(ibuf, 0, k), part(ibuf, 2, k), by_low))
+
+    for k in chunks:
+        y_copies[k].wait_recv()
+        core_copies.append(push(part(tbuf, 1, k), part(tbuf, 5, k), by_core))
     diagonal_copies = []
-    for copy, span in zip(high_copies, spans):
-        copy.wait_recv()
-        diagonal_copies.append(push(slot(tbuf, 4, span), slot(tbuf, 6, span), by_y))
-        core_copies.append(push(slot(tbuf, 4, span), slot(tbuf, 5, span), by_core))
-    y_copy.wait_recv()
-    core_copies.append(push(slot(tbuf, 2), slot(tbuf, 3), by_core))
-    for copy, span in zip(diagonal_copies, spans):
-        copy.wait_recv()
-        core_copies.append(push(slot(tbuf, 6, span), slot(tbuf, 7, span), by_core))
+    image_diagonals = []
+    for k in chunks:
+        if k % 2 == 0:
+            x_copies[k].wait_recv()
+            image_diagonals.append(push(part(ibuf, 1, k), part(ibuf, 3, k), by_low))
+        else:
+            low_copies[k].wait_recv()
+            image_diagonals.append(push(part(ibuf, 2, k), part(ibuf, 3, k), by_x))
+        high_copies[k].wait_recv()
+        diagonal_copies.append(push(part(tbuf, 2, k), part(tbuf, 3, k), by_y))
+        core_copies.append(push(part(tbuf, 2, k), part(tbuf, 6, k), by_core))
+    for k in chunks:
+        diagonal_copies[k].wait_recv()
+        core_copies.append(push(part(tbuf, 3, k), part(tbuf, 7, k), by_core))
     arrived(core_copies)
-    arrived(image_copies)
+    for k in chunks:
+        (low_copies if k % 2 == 0 else x_copies)[k].wait_recv()
+    arrived(image_diagonals)
 
     scale = scale_ref[0, 0]
     shift = shift_ref[0, 0]
@@ -700,99 +729,105 @@
         weight = scale * jax.nn.sigmoid(jnp.where(same, -energy, energy))
         weights[:, first : first + group] = jnp.where(same, -weight, weight).astype(BF16)
 
+    d_part[of(2), :] = dot(weights[of(3), :], tbuf[...]).astype(BF16)
+    through = [
+        push(part(d_part, 2, k), part(d_through, 0, k), by_x if k % 2 == 0 else by_low) for k in chunks
+    ]
+    d_near[...] = dot(weights[share : 3 * share, :], tbuf[...])
     dir_copies = []
-    for span in spans:
-        total = dot(weights[...], tbuf[:, span])
-        d_own[:, span] = total[:share]
-        d_part[:, span] = total[share:].astype(BF16)
-        for at, partner in ((2, by_both), (0, by_x), (1, by_low)):
-            dir_copies.append(push(slot(d_part, at, span), slot(d_land, at, span), partner))
-
-    core_copies = []
-    for span in spans:
-        total = dot_tn(weights[...], ibuf[:, span])
-        for at in range(4):
-            first = 2 * at * share
-            s_own[at, :, span] = total[first : first + share]
-            c_part[at * share : (at + 1) * share, span] = total[
-                first + share : first + 2 * share
-            ].astype(BF16)
-        core_copies.append(push(c_part.at[:, span], c_land.at[:, span], by_core))
-    diagonal_copies = []
-    for copy, span in zip(core_copies, spans):
-        copy.wait_recv()
-        for at in range(4):
-            total = s_own[at, :, span] + c_land[at * share : (at + 1) * share, span].astype(F32)
-            if at % 2:
-                first = (at // 2) * share
-                y_part[first : first + share, span] = total.astype(BF16)
-            else:
-                s_own[at, :, span] = total
-        diagonal_copies.append(push(slot(y_part, 1, span), slot(y_land, 1, span), by_y))
-    y_copies = [push(slot(y_part, 0, span), slot(y_land, 0, span), by_y) for span in spans]
+    for k in chunks:
+        at = 0 if k % 2 == 0 else 1
+        d_part[lines(at, k)] = d_near[lines(at, k)].astype(BF16)
+        dir_copies.append(push(part(d_part, at, k), part(d_land, at, k), (by_x, by_low)[at]))
+
+    c_part[...] = dot_tn(weights[:, 4 * share :], ibuf[...]).astype(BF16)
+    core_copies = [push(block(c_part, at), block(c_land, at), by_core) for at in (3, 1, 2, 0)]
+    s_own[...] = dot_tn(weights[:, : 4 * share], ibuf[...])
+    core_copies[0].wait_recv()
+    y_part[of(1), :] = (s_own[of(3), :] + c_land[of(3), :].astype(F32)).astype(BF16)
+    diagonal_copies = [push(part(y_part, 1, k), part(y_land, 1, k), by_y) for k in chunks]
+    core_copies[1].wait_recv()
+    y_part[of(0), :] = (s_own[of(1), :] + c_land[of(1), :].astype(F32)).astype(BF16)
+    y_copies = [push(part(y_part, 0, k), part(y_land, 0, k), by_y) for k in chunks]
+    for k in chunks:
+        at = 1 if k % 2 == 0 else 0
+        through[k].wait_recv()
+        d_part[lines(at, k)] = (d_near[lines(at, k)] + d_through[lines(0, k)].astype(F32)).astype(BF16)
+        dir_copies.append(push(part(d_part, at, k), part(d_land, at, k), (by_x, by_low)[at]))
+    d_own[...] = dot(weights[of(0), :], tbuf[...])
+    arrived(core_copies[2:])
+    for at in (0, 2):
+        s_own[of(at), :] = s_own[of(at), :] + c_land[of(at), :].astype(F32)
     high_copies = []
-    for copy, span in zip(diagonal_copies, spans):
-        copy.wait_recv()
-        h_part[:, span] = (s_own[2, :, span] + y_land[share:, span].astype(F32)).astype(BF16)
-        high_copies.append(push(h_part.at[:, span], h_land.at[:, span], by_high))
+    for k in chunks:
+        diagonal_copies[k].wait_recv()
+        h_part[lines(0, k)] = (s_own[lines(2, k)] + y_land[lines(1, k)].astype(F32)).astype(BF16)
+        high_copies.append(push(part(h_part, 0, k), part(h_land, 0, k), by_high))
 
     arrived(dir_copies)
-    image_dir = d_own[...]
-    for at in range(3):
-        image_dir = image_dir + d_land[at * share : (at + 1) * share, :].astype(F32)
-    grad_out = norm_back(image_dir, ibuf[:share], inv_image)
-    g_part[...] = grad_out.astype(BF16)
+    for k in chunks:
+        total = d_own[lines(0, k)] + d_land[lines(0, k)].astype(F32) + d_land[lines(1, k)].astype(F32)
+        g_part[lines(0, k)] = norm_back(total, ibuf[lines(0, k)], inv_image[k]).astype(BF16)
     grad_copy = push(g_part, g_land, by_x)
 
+    gain = gain_ref[...].reshape(1, width)
+    mine_first = head == 0
+    gains = jnp.where(mine_first, gain[:, :cols], gain[:, cols:])
+
+    def backward(at, upstream):
+        grad_b = upstream[...]
+        for first, size in tiles:
+            span = slice(first, first + size)
+            values[of(at), span] = (dot_nt(grad_b, exit_[span, :]) * slope[of(at), span]).astype(BF16)
+        total = dot(values[of(at), :], entry[...])
+        lower = total[:, :cols]
+        upper = total[:, cols:]
+        n_part[of(at), :cols] = jnp.where(mine_first, upper, lower).astype(BF16)
+        grad_normed = jnp.where(mine_first, lower, upper)
+        scaled = total * gain
+        one_sum = jnp.sum(scaled, axis=-1, keepdims=True)
+        two_sum = jnp.sum(scaled * centred_ref[of(at), :], axis=-1, keepdims=True)
+        lane = lax.broadcasted_iota(jnp.int32, (share, n_part.shape[1] - cols), 1)
+        packed = jnp.zeros(lane.shape, F32)
+        for place, term in enumerate(split_three(one_sum) + split_three(two_sum)):
+            packed = jnp.where(lane == place, term.astype(F32), packed)
+        n_part[of(at), cols:] = packed.astype(BF16)
+        return push(block(n_part, at), block(n_land, 1 - at), by_x), grad_normed, one_sum, two_sum
+
+    def finish(at, upstream, grad_normed, one_sum, two_sum):
+        grad_float = upstream[...].astype(F32)
+        grad_float = jnp.where(mine_first, grad_float[:, :cols], grad_float[:, cols:])
+        centred = centred_ref[of(at), :]
+        centred = jnp.where(mine_first, centred[:, :cols], centred[:, cols:])
+        grad_normed = grad_normed + n_land[of(at), :cols].astype(F32)
+        sums = n_land[of(at), cols:].astype(F32)
+        mean_one = (one_sum + (sums[:, 0:1] + sums[:, 1:2] + sums[:, 2:3])) * (1.0 / width)
+        mean_two = (two_sum + (sums[:, 3:4] + sums[:, 4:5] + sums[:, 5:6])) * (1.0 / width)
+        result = grad_float + inv_std[of(at)] * (grad_normed * gains - mean_one - centred * mean_two)
+        out_image[(own_rows, other_rows)[at], :] = result
+
+    text_copies = []
+
+    def text_back(k):
+        high_copies[k].wait_recv()
+        y_copies[k].wait_recv()
+        total = s_own[lines(0, k)] + y_land[lines(0, k)].astype(F32) + h_land[lines(0, k)].astype(F32)
+        gt_part[lines(0, k)] = norm_back(total, tbuf[lines(0, k)], inv_text[k]).astype(BF16)
+        text_copies.append(push(part(gt_part, 0, k), part(gt_land, 0, k), by_x))
+
+    own_copy, *own_terms = backward(0, g_part)
+    text_back(0)
     grad_copy.wait_recv()
-    grad_b = jnp.concatenate([g_part[...], g_land[...]], axis=0)
-    for first, size in tiles:
-        span = slice(first, first + size)
-        values[:, span] = (dot_nt(grad_b, exit_[span, :]) * slope[:, span]).astype(BF16)
-    total = dot(values[...], entry[...])
-    mine_first = head == 0
-    lower = total[:, :cols]
-    upper = total[:, cols:]
-    theirs = jnp.where(mine_first, upper, lower).astype(BF16)
-    n_part[:share, :cols] = theirs[share:]
-    n_part[share:, :cols] = theirs[:share]
-    grad_normed = jnp.where(mine_first, lower, upper)
-    scaled = total * gain_ref[...].reshape(1, width)
-    centred = centred_ref[...]
-    one_sum = jnp.sum(scaled, axis=-1, keepdims=True)
-    two_sum = jnp.sum(scaled * centred, axis=-1, keepdims=True)
-    lane = lax.broadcasted_iota(jnp.int32, (rows, n_part.shape[1] - cols), 1)
-    packed = jnp.zeros(lane.shape, F32)
-    for at, term in enumerate(split_three(one_sum) + split_three(two_sum)):
-        packed = jnp.where(lane == at, term.astype(F32), packed)
-    n_part[:share, cols:] = packed[share:].astype(BF16)
-    n_part[share:, cols:] = packed[:share].astype(BF16)
-    norm_copy = push(n_part, n_land, by_x)
-
-    arrived(y_copies)
-    arrived(high_copies)
-    text_dir = s_own[0] + y_land[:share, :].astype(F32) + h_land[...].astype(F32)
-    gt_part[...] = norm_back(text_dir, tbuf[:share], inv_text).astype(BF16)
-    text_copy = push(gt_part, gt_land, by_x)
-
-    norm_copy.wait_recv()
-    gains = gain_ref[...].reshape(1, width)
-    gains = jnp.where(mine_first, gains[:, :cols], gains[:, cols:])
-    centred = jnp.where(mine_first, centred[:, :cols], centred[:, cols:])
-    grad_float = grad_b.astype(F32)
-    grad_float = jnp.where(mine_first, grad_float[:, :cols], grad_float[:, cols:])
-    grad_normed = grad_normed + n_land[:, :cols].astype(F32)
-    sums = n_land[:, cols:].astype(F32)
-    mean_one = (one_sum + (sums[:, 0:1] + sums[:, 1:2] + sums[:, 2:3])) * (1.0 / width)
-    mean_two = (two_sum + (sums[:, 3:4] + sums[:, 4:5] + sums[:, 5:6])) * (1.0 / width)
-    result = grad_float + inv_std * (grad_normed * gains - mean_one - centred * mean_two)
-    out_image[own_rows, :] = result[:share]
-    out_image[other_rows, :] = result[share:]
-
-    text_copy.wait_recv()
-    result = dot_nt(jnp.concatenate([gt_part[...], gt_land[...]], axis=0), mapping[...])
-    out_text[own_rows, :] = result[:share]
-    out_text[other_rows, :] = result[share:]
+    their_copy, *their_terms = backward(1, g_land)
+    for k in chunks[1:]:
+        text_back(k)
+    own_copy.wait_recv()
+    finish(1, g_land, *their_terms)
+    out_text[own_rows, :] = dot_nt(gt_part[...], mapping[...])
+    their_copy.wait_recv()
+    finish(0, g_part, *own_terms)
+    arrived(text_copies)
+    out_text[other_rows, :] = dot_nt(gt_land[...], mapping[...])
     for copy in pending:
         copy.wait_send()
 
@@ -811,7 +846,7 @@
     def blocks(count, dtype=BF16):
         return pltpu.VMEM((count * share, width), dtype)
 
-    loads = 5 + 2 * pl.cdiv(hidden, TILE)
+    loads = 6 + 2 * pl.cdiv(hidden, TILE)
     copies = 64
     extended = 128 * (cols // 128 + 1)
     return pl.pallas_call(
@@ -820,11 +855,12 @@
             jax.ShapeDtypeStruct((rows, cols), F32),
             jax.ShapeDtypeStruct((rows, mapping.shape[0]), F32),
         ),
-        in_specs=[anywhere, anywhere, vmem, anywhere, anywhere, anywhere, smem, smem],
+        in_specs=[anywhere] * 6 + [smem, smem],
         out_specs=(vmem, vmem),
         scratch_shapes=[
             pltpu.VMEM(pic.shape, BF16),
             pltpu.VMEM(cap.shape, BF16),
+            pltpu.VMEM(gain.shape, F32),
             pltpu.VMEM(flipped.shape, BF16),
             pltpu.VMEM(exit_.shape, BF16),
             pltpu.VMEM(mapping.shape, BF16),
@@ -843,11 +879,13 @@
             blocks(4),
             pltpu.VMEM((4 * share, 8 * share), BF16),
             blocks(1, F32),
+            blocks(2, F32),
             blocks(3),
-            blocks(3),
-            blocks(1),
-            blocks(1),
-            pltpu.VMEM((4, share, width), F32),
+            blocks(1),
+            blocks(2),
+            blocks(1),
+            blocks(1),
+            blocks(4, F32),
             blocks(4),
             blocks(4),
             blocks(2),

time: 74.9 us -> 65.6 us (0.88)
  Pallas kernels: 69.1 us -> 59.8 us
    pallas_call x1, Pallas kernels: 69.1 us -> 59.8 us  [square_device(): pl.pallas_call(square_body, out_shape=(jax.ShapeDtypeStruct((rows, cols),...]
where the time goes in v2:
time: 65.6 us; the launch traced here: 65.4 us
  Pallas kernels  59.8 us (91%)
  local copies, waits for them, and re-layouts  3.68 us (6%)
  between operations  1.93 us (3%)
    pallas_call x1, Pallas kernels, square_device(): pl.pallas_call(square_body, out_shape=(jax.ShapeDtypeStruct((rows, cols),...  59.8 us
    unnamed x2, local copies, waits for them, and re-layouts  3.68 us

profile of v2, /device:TPU:0, one launch (start us, length us, event | category | flops | bytes accessed | tf_op | source)
XLA Modules:
  0.0 65.4 jit_solution(14028901092743626875)
XLA Ops:
  1.9 59.8 %contrastive_square.1 = (f32[192,576]{1,0:T(8,128)}, f32[192,576]{1,0:T(8,128)}) custom-call(bf16[192,1152]{1,0:T(8,128)(2,1)} %pic_hbm.1, bf16[192,576]{1,0:T(8,128)(2,1)} %cap_hbm.1, f32[1152]{0:T(1024)} %gain_hbm.1, bf16[2152,1152]{1,0:T(8,128)(2,1)} %bitcast.5, bf16[2152,1152]{1,0:T(8,128)(2,1)} %exit_hbm.1, bf16[576,1152]{1,0:T(8,128)(2,1)} %map_hbm.1, ...), custom_call_target="tpu_custom_call" | custom-call | tf_op jit(solution)/shard_map/contrastive_square/pallas_call | solution.py:852
  61.7 1.8 %copy.14 = f32[192,576]{1,0:T(8,128)} copy(f32[192,576]{1,0:T(8,128)} %get-tuple-element.4) | data formatting | bytes 884736
  63.6 1.8 %copy.15 = f32[192,576]{1,0:T(8,128)} copy(f32[192,576]{1,0:T(8,128)} %get-tuple-element.5) | data formatting | bytes 884736

commit v3 on v2

--- a/solution.py
+++ b/solution.py
@@ -504,10 +504,15 @@
     entry_hbm,
     exit_hbm,
     map_hbm,
+    scale_hbm,
+    shift_hbm,
+    out_image_hbm,
+    out_text_hbm,
     scale_ref,
     shift_ref,
     out_image,
     out_text,
+    store_sem,
     pic,
     cap,
     gain_ref,
@@ -564,9 +569,10 @@
     own_rows = pl.ds(pl.multiple_of(head * share, 16), share)
     other_rows = pl.ds(pl.multiple_of(other * share, 16), share)
     tiles = [(first, min(TILE, hidden - first)) for first in range(0, hidden, TILE)]
-    chunk = share // 2 if share % 32 == 0 else share
+    chunk = share // 3 if share % 48 == 0 else share
     chunks = range(share // chunk)
     spans = [slice(first, min(first + TILE, width)) for first in range(0, width, TILE)]
+    x_first = [k == 2 for k in chunks]
 
     def block(ref, at):
         return ref.at[pl.ds(at * share, share)]
@@ -598,12 +604,11 @@
         load(pic_hbm.at[own_rows], block(pic, 0)),
         load(pic_hbm.at[other_rows], block(pic, 1)),
         load(gain_hbm, gain_ref),
+        load(scale_hbm, scale_ref),
+        load(shift_hbm, shift_ref),
     ]
     entry_loads = [
         load(entry_hbm.at[pl.ds(first, size)], entry.at[pl.ds(first, size)]) for first, size in tiles
-    ]
-    exit_loads = [
-        load(exit_hbm.at[pl.ds(first, size)], exit_.at[pl.ds(first, size)]) for first, size in tiles
     ]
 
     barrier = pltpu.get_barrier_semaphore()
@@ -637,6 +642,9 @@
     pl.semaphore_wait(barrier, len(partners))
     text_partials = [push(part(t_part, 0, k), part(t_land, 0, k), by_x) for k in chunks]
     t_own[...] = dot(cap[:share], mapping[...])
+    exit_loads = [
+        load(exit_hbm.at[pl.ds(first, size)], exit_.at[pl.ds(first, size)]) for first, size in tiles
+    ]
 
     for copy in pic_loads:
         copy.wait()
@@ -649,32 +657,37 @@
     centred_ref[...] = centred
     normed[...] = (centred * gain).astype(BF16)
 
-    for (first, size), copy in zip(tiles, entry_loads):
+    def unit_rows(own, land, k, dst):
+        total = own[lines(0, k)] + land[lines(0, k)].astype(F32)
+        inverse = lax.rsqrt(jnp.sum(total * total, axis=-1, keepdims=True) + 1e-06)
+        dst[lines(0, k)] = (total * inverse).astype(BF16)
+        return inverse
+
+    inv_text = []
+    high_copies = []
+    y_copies = []
+    early_copies = []
+    late_copies = []
+
+    def send_high(k):
+        high_copies.append(push(part(tbuf, 0, k), part(tbuf, 4, k), by_high))
+
+    def text_chunk(k):
+        text_partials[k].wait_recv()
+        inv_text.append(unit_rows(t_own, t_land, k, tbuf))
+        if k < 2:
+            send_high(k)
+        y_copies.append(push(part(tbuf, 0, k), part(tbuf, 1, k), by_y))
+        early_copies.append(push(part(tbuf, 0, k), part(tbuf, 2, k), by_core))
+
+    for at, ((first, size), copy) in enumerate(zip(tiles, entry_loads)):
         copy.wait()
         span = slice(first, first + size)
         value, grad = gelu_pair(dot_nt(normed[...], entry[span, :]))
         slope[:, span] = grad
         values[:, span] = value.astype(BF16)
-
-    def unit_rows(own, land, k, dst):
-        total = own[lines(0, k)] + land[lines(0, k)].astype(F32)
-        inverse = lax.rsqrt(jnp.sum(total * total, axis=-1, keepdims=True) + 1e-06)
-        dst[lines(0, k)] = (total * inverse).astype(BF16)
-        return inverse
-
-    inv_text = []
-    high_copies = []
-    y_copies = []
-    core_copies = []
-
-    def text_chunk(k):
-        text_partials[k].wait_recv()
-        inv_text.append(unit_rows(t_own, t_land, k, tbuf))
-        high_copies.append(push(part(tbuf, 0, k), part(tbuf, 2, k), by_high))
-        y_copies.append(push(part(tbuf, 0, k), part(tbuf, 1, k), by_y))
-        core_copies.append(push(part(tbuf, 0, k), part(tbuf, 4, k), by_core))
-
-    text_chunk(0)
+        if at == len(tiles) - 2:
+            text_chunk(0)
     for copy in exit_loads:
         copy.wait()
     for span in spans:
@@ -693,92 +706,129 @@
         inv_image.append(unit_rows(i_own, i_land, k, ibuf))
         x_copies.append(push(part(ibuf, 0, k), part(ibuf, 1, k), by_x))
         low_copies.append(push(part(ibuf, 0, k), part(ibuf, 2, k), by_low))
+        if k == 2:
+            send_high(2)
 
     for k in chunks:
         y_copies[k].wait_recv()
-        core_copies.append(push(part(tbuf, 1, k), part(tbuf, 5, k), by_core))
+        early_copies.append(push(part(tbuf, 1, k), part(tbuf, 3, k), by_core))
     diagonal_copies = []
-    image_diagonals = []
+    image_copies = []
     for k in chunks:
-        if k % 2 == 0:
+        if x_first[k]:
             x_copies[k].wait_recv()
-            image_diagonals.append(push(part(ibuf, 1, k), part(ibuf, 3, k), by_low))
+            image_copies.append(push(part(ibuf, 1, k), part(ibuf, 3, k), by_low))
         else:
             low_copies[k].wait_recv()
-            image_diagonals.append(push(part(ibuf, 2, k), part(ibuf, 3, k), by_x))
+            image_copies.append(push(part(ibuf, 2, k), part(ibuf, 3, k), by_x))
         high_copies[k].wait_recv()
-        diagonal_copies.append(push(part(tbuf, 2, k), part(tbuf, 3, k), by_y))
-        core_copies.append(push(part(tbuf, 2, k), part(tbuf, 6, k), by_core))
+        diagonal_copies.append(push(part(tbuf, 4, k), part(tbuf, 5, k), by_y))
+        late_copies.append(push(part(tbuf, 4, k), part(tbuf, 6, k), by_core))
+    for k in chunks:
+        (low_copies if x_first[k] else x_copies)[k].wait_recv()
+    arrived(image_copies)
+    arrived(early_copies)
+
+    scale = scale_ref[0, 0]
+    shift = shift_ref[0, 0]
+    early = slice(0, 4 * share)
+    late = slice(4 * share, 8 * share)
+
+    def weigh(texts, paired):
+        energy = scale * dot_nt(ibuf[...], tbuf[texts, :]) + shift
+        if paired:
+            row = lax.broadcasted_iota(jnp.int32, energy.shape, 0)
+            column = lax.broadcasted_iota(jnp.int32, energy.shape, 1)
+            same = jnp.logical_and(row == column, row < share)
+            weight = scale * jax.nn.sigmoid(jnp.where(same, -energy, energy))
+            weight = jnp.where(same, -weight, weight)
+        else:
+            weight = scale * jax.nn.sigmoid(energy)
+        weights[:, texts] = weight.astype(BF16)
+
+    weigh(early, True)
+    c_part[: 2 * share] = dot_tn(weights[:, 2 * share : 4 * share], ibuf[...]).astype(BF16)
+    core_early = push(c_part.at[pl.ds(0, 2 * share)], c_land.at[pl.ds(0, 2 * share)], by_core)
+    s_own[: 2 * share] = dot_tn(weights[:, : 2 * share], ibuf[...])
+    d_near[...] = dot(weights[:, early], tbuf[early, :])
+
     for k in chunks:
         diagonal_copies[k].wait_recv()
-        core_copies.append(push(part(tbuf, 3, k), part(tbuf, 7, k), by_core))
-    arrived(core_copies)
+        late_copies.append(push(part(tbuf, 5, k), part(tbuf, 7, k), by_core))
+    core_early.wait_recv()
+    y_part[of(0), :] = (s_own[of(1), :] + c_land[of(1), :].astype(F32)).astype(BF16)
+    s_own[of(0), :] = s_own[of(0), :] + c_land[of(0), :].astype(F32)
+    arrived(late_copies)
+
+    weigh(late, False)
+
+    d_part[of(2), :] = (d_near[of(3), :] + dot(weights[of(3), late], tbuf[late, :])).astype(BF16)
+    through = [
+        push(part(d_part, 2, k), part(d_through, 0, k), by_x if x_first[k] else by_low) for k in chunks
+    ]
+    d_near[share : 3 * share] += dot(weights[share : 3 * share, late], tbuf[late, :])
+    from_x = [None for k in chunks]
+    from_low = [None for k in chunks]
+
+    def send_dir(at, k):
+        copy = push(part(d_part, at, k), part(d_land, at, k), (by_x, by_low)[at])
+        (from_x, from_low)[at][k] = copy
+
     for k in chunks:
-        (low_copies if k % 2 == 0 else x_copies)[k].wait_recv()
-    arrived(image_diagonals)
-
-    scale = scale_ref[0, 0]
-    shift = shift_ref[0, 0]
-    texts = 8 * share
-    group = texts // 3 if texts % 384 == 0 else texts
-    for first in range(0, texts, group):
-        energy = scale * dot_nt(ibuf[...], tbuf[first : first + group, :]) + shift
-        row = lax.broadcasted_iota(jnp.int32, energy.shape, 0)
-        column = lax.broadcasted_iota(jnp.int32, energy.shape, 1) + first
-        same = jnp.logical_and(row == column, row < share)
-        weight = scale * jax.nn.sigmoid(jnp.where(same, -energy, energy))
-        weights[:, first : first + group] = jnp.where(same, -weight, weight).astype(BF16)
-
-    d_part[of(2), :] = dot(weights[of(3), :], tbuf[...]).astype(BF16)
-    through = [
-        push(part(d_part, 2, k), part(d_through, 0, k), by_x if k % 2 == 0 else by_low) for k in chunks
-    ]
-    d_near[...] = dot(weights[share : 3 * share, :], tbuf[...])
-    dir_copies = []
-    for k in chunks:
-        at = 0 if k % 2 == 0 else 1
-        d_part[lines(at, k)] = d_near[lines(at, k)].astype(BF16)
-        dir_copies.append(push(part(d_part, at, k), part(d_land, at, k), (by_x, by_low)[at]))
-
-    c_part[...] = dot_tn(weights[:, 4 * share :], ibuf[...]).astype(BF16)
-    core_copies = [push(block(c_part, at), block(c_land, at), by_core) for at in (3, 1, 2, 0)]
-    s_own[...] = dot_tn(weights[:, : 4 * share], ibuf[...])
-    core_copies[0].wait_recv()
+        at = 0 if x_first[k] else 1
+        d_part[lines(at, k)] = d_near[lines(at + 1, k)].astype(BF16)
+        send_dir(at, k)
+
+    c_part[2 * share :] = dot_tn(weights[:, 6 * share :], ibuf[...]).astype(BF16)
+    core_late = [push(block(c_part, at), block(c_land, at), by_core) for at in (3, 2)]
+    s_own[2 * share :] = dot_tn(weights[:, 4 * share : 6 * share], ibuf[...])
+    core_late[0].wait_recv()
     y_part[of(1), :] = (s_own[of(3), :] + c_land[of(3), :].astype(F32)).astype(BF16)
     diagonal_copies = [push(part(y_part, 1, k), part(y_land, 1, k), by_y) for k in chunks]
-    core_copies[1].wait_recv()
-    y_part[of(0), :] = (s_own[of(1), :] + c_land[of(1), :].astype(F32)).astype(BF16)
     y_copies = [push(part(y_part, 0, k), part(y_land, 0, k), by_y) for k in chunks]
     for k in chunks:
-        at = 1 if k % 2 == 0 else 0
+        at = 1 if x_first[k] else 0
         through[k].wait_recv()
-        d_part[lines(at, k)] = (d_near[lines(at, k)] + d_through[lines(0, k)].astype(F32)).astype(BF16)
-        dir_copies.append(push(part(d_part, at, k), part(d_land, at, k), (by_x, by_low)[at]))
-    d_own[...] = dot(weights[of(0), :], tbuf[...])
-    arrived(core_copies[2:])
-    for at in (0, 2):
-        s_own[of(at), :] = s_own[of(at), :] + c_land[of(at), :].astype(F32)
+        total = d_near[lines(at + 1, k)] + d_through[lines(0, k)].astype(F32)
+        d_part[lines(at, k)] = total.astype(BF16)
+        send_dir(at, k)
+    d_own[...] = d_near[of(0), :] + dot(weights[of(0), late], tbuf[late, :])
+    core_late[1].wait_recv()
+    s_own[of(2), :] = s_own[of(2), :] + c_land[of(2), :].astype(F32)
     high_copies = []
     for k in chunks:
         diagonal_copies[k].wait_recv()
         h_part[lines(0, k)] = (s_own[lines(2, k)] + y_land[lines(1, k)].astype(F32)).astype(BF16)
         high_copies.append(push(part(h_part, 0, k), part(h_land, 0, k), by_high))
 
-    arrived(dir_copies)
+    grad_copies = []
     for k in chunks:
+        from_x[k].wait_recv()
+        from_low[k].wait_recv()
         total = d_own[lines(0, k)] + d_land[lines(0, k)].astype(F32) + d_land[lines(1, k)].astype(F32)
         g_part[lines(0, k)] = norm_back(total, ibuf[lines(0, k)], inv_image[k]).astype(BF16)
-    grad_copy = push(g_part, g_land, by_x)
+        grad_copies.append(push(part(g_part, 0, k), part(g_land, 0, k), by_x))
 
     gain = gain_ref[...].reshape(1, width)
     mine_first = head == 0
     gains = jnp.where(mine_first, gain[:, :cols], gain[:, cols:])
-
-    def backward(at, upstream):
+    stores = []
+
+    def store(src, dst, first, begin, count):
+        start = pl.multiple_of(begin, 16)
+        copy = pltpu.make_async_copy(
+            src.at[pl.ds(first, count)], dst.at[pl.ds(start, count)], store_sem.at[len(stores)]
+        )
+        copy.start()
+        stores.append(copy)
+
+    def backward_exit(at, upstream):
         grad_b = upstream[...]
-        for first, size in tiles:
-            span = slice(first, first + size)
+        for begin, size in tiles:
+            span = slice(begin, begin + size)
             values[of(at), span] = (dot_nt(grad_b, exit_[span, :]) * slope[of(at), span]).astype(BF16)
+
+    def backward_entry(at):
         total = dot(values[of(at), :], entry[...])
         lower = total[:, :cols]
         upper = total[:, cols:]
@@ -792,19 +842,21 @@
         for place, term in enumerate(split_three(one_sum) + split_three(two_sum)):
             packed = jnp.where(lane == place, term.astype(F32), packed)
         n_part[of(at), cols:] = packed.astype(BF16)
-        return push(block(n_part, at), block(n_land, 1 - at), by_x), grad_normed, one_sum, two_sum
+        return push(block(n_part, at), block(n_land, 1 - at), by_x), (grad_normed, one_sum, two_sum)
 
     def finish(at, upstream, grad_normed, one_sum, two_sum):
+        lines = of(at)
         grad_float = upstream[...].astype(F32)
         grad_float = jnp.where(mine_first, grad_float[:, :cols], grad_float[:, cols:])
-        centred = centred_ref[of(at), :]
+        centred = centred_ref[lines, :]
         centred = jnp.where(mine_first, centred[:, :cols], centred[:, cols:])
-        grad_normed = grad_normed + n_land[of(at), :cols].astype(F32)
-        sums = n_land[of(at), cols:].astype(F32)
+        grad_normed = grad_normed + n_land[lines, :cols].astype(F32)
+        sums = n_land[lines, cols:].astype(F32)
         mean_one = (one_sum + (sums[:, 0:1] + sums[:, 1:2] + sums[:, 2:3])) * (1.0 / width)
         mean_two = (two_sum + (sums[:, 3:4] + sums[:, 4:5] + sums[:, 5:6])) * (1.0 / width)
-        result = grad_float + inv_std[of(at)] * (grad_normed * gains - mean_one - centred * mean_two)
-        out_image[(own_rows, other_rows)[at], :] = result
+        result = grad_float + inv_std[lines] * (grad_normed * gains - mean_one - centred * mean_two)
+        out_image[lines, :] = result
+        store(out_image, out_image_hbm, at * share, (head, other)[at] * share, share)
 
     text_copies = []
 
@@ -815,21 +867,49 @@
         gt_part[lines(0, k)] = norm_back(total, tbuf[lines(0, k)], inv_text[k]).astype(BF16)
         text_copies.append(push(part(gt_part, 0, k), part(gt_land, 0, k), by_x))
 
-    own_copy, *own_terms = backward(0, g_part)
+    backward_exit(0, g_part)
+    own_copy, own_terms = backward_entry(0)
+    arrived(grad_copies)
+    backward_exit(1, g_land)
     text_back(0)
-    grad_copy.wait_recv()
-    their_copy, *their_terms = backward(1, g_land)
+    their_copy, their_terms = backward_entry(1)
     for k in chunks[1:]:
         text_back(k)
     own_copy.wait_recv()
     finish(1, g_land, *their_terms)
-    out_text[own_rows, :] = dot_nt(gt_part[...], mapping[...])
+    out_text[:share, :] = dot_nt(gt_part[...], mapping[...])
+    store(out_text, out_text_hbm, 0, head * share, share)
     their_copy.wait_recv()
     finish(0, g_part, *own_terms)
     arrived(text_copies)
-    out_text[other_rows, :] = dot_nt(gt_land[...], mapping[...])
+    out_text[share:, :] = dot_nt(gt_land[...], mapping[...])
+    store(out_text, out_text_hbm, share, other * share, share)
     for copy in pending:
         copy.wait_send()
+    for copy in stores:
+        copy.wait()
+
+
+def hand_over(image_hbm, text_hbm, out_image, out_text, image, text, in_sem, out_sem):
+    rows = image.shape[0]
+    count = 4 if rows % 32 == 0 else 1
+    size = rows // count
+    pieces = [
+        (src, mid, dst, pl.ds(at * size, size))
+        for at in range(count)
+        for src, mid, dst in ((image_hbm, image, out_image), (text_hbm, text, out_text))
+    ]
+    ins = []
+    outs = []
+    for at, (src, mid, dst, lines) in enumerate(pieces):
+        ins.append(pltpu.make_async_copy(src.at[lines], mid.at[lines], in_sem.at[at]))
+        outs.append(pltpu.make_async_copy(mid.at[lines], dst.at[lines], out_sem.at[at]))
+        ins[at].start()
+    for taken, given in zip(ins, outs):
+        taken.wait()
+        given.start()
+    for given in outs:
+        given.wait()
 
 
 def square_device(pic, cap, gain, entry, exit_, mapping, scale, shift):
@@ -839,25 +919,29 @@
     hidden = entry.shape[1]
     flipped = entry.T
     anywhere = pl.BlockSpec(memory_space=pl.ANY)
-    vmem = pl.BlockSpec(memory_space=pltpu.VMEM)
-    smem = pl.BlockSpec(memory_space=pltpu.SMEM)
     dma = pltpu.SemaphoreType.DMA
 
     def blocks(count, dtype=BF16):
         return pltpu.VMEM((count * share, width), dtype)
 
-    loads = 6 + 2 * pl.cdiv(hidden, TILE)
-    copies = 64
+    loads = 8 + 2 * pl.cdiv(hidden, TILE)
+    copies = 66
     extended = 128 * (cols // 128 + 1)
-    return pl.pallas_call(
+    results = (
+        jax.ShapeDtypeStruct((rows, cols), F32),
+        jax.ShapeDtypeStruct((rows, mapping.shape[0]), F32),
+    )
+    image, text = pl.pallas_call(
         square_body,
-        out_shape=(
-            jax.ShapeDtypeStruct((rows, cols), F32),
-            jax.ShapeDtypeStruct((rows, mapping.shape[0]), F32),
-        ),
-        in_specs=[anywhere] * 6 + [smem, smem],
-        out_specs=(vmem, vmem),
+        out_shape=results,
+        in_specs=[anywhere] * 8,
+        out_specs=(anywhere, anywhere),
         scratch_shapes=[
+            pltpu.SMEM((1, 1), F32),
+            pltpu.SMEM((1, 1), F32),
+            pltpu.VMEM((rows, cols), F32),
+            pltpu.VMEM((rows, mapping.shape[0]), F32),
+            dma((4,)),
             pltpu.VMEM(pic.shape, BF16),
             pltpu.VMEM(cap.shape, BF16),
             pltpu.VMEM(gain.shape, F32),
@@ -879,7 +963,7 @@
             blocks(4),
             pltpu.VMEM((4 * share, 8 * share), BF16),
             blocks(1, F32),
-            blocks(2, F32),
+            blocks(4, F32),
             blocks(3),
             blocks(1),
             blocks(2),
@@ -913,6 +997,15 @@
         scale.reshape(1, 1),
         shift.reshape(1, 1),
     )
+    return pl.pallas_call(
+        hand_over,
+        out_shape=results,
+        in_specs=[anywhere, anywhere],
+        out_specs=(anywhere, anywhere),
+        scratch_shapes=[pltpu.VMEM(r.shape, F32) for r in results] + [dma((8,)), dma((8,))],
+        compiler_params=pltpu.CompilerParams(vmem_limit_bytes=60 * 2**20),
+        name="hand_over",
+    )(image, text)
 
 
 def solution(mesh):

time: 65.6 us -> 62.7 us (0.956)
  local copies, waits for them, and re-layouts: 3.68 us -> 0 us
  Pallas kernels: 59.8 us -> 60.6 us
    unnamed x2 -> x0, local copies, waits for them, and re-layouts: 3.68 us -> none
    pallas_call x1 -> x2, Pallas kernels: 59.8 us -> 60.6 us  [the longest x1 58.6 us: square_device(): pl.pallas_call(square_body, out_shape=results, in_specs=[anywhere] * 8, o...]
where the time goes in v3:
time: 62.7 us; the launch traced here: 62.6 us
  Pallas kernels  60.6 us (97%)
  between operations  1.93 us (3%)
    pallas_call x1, Pallas kernels, square_device(): pl.pallas_call(square_body, out_shape=results, in_specs=[anywhere] * 8, o...  58.6 us
    pallas_call x1, Pallas kernels, square_device(): pl.pallas_call(hand_over, out_shape=results, in_specs=[anywhere, anywhere...  2.07 us

profile of v3, /device:TPU:0, one launch (start us, length us, event | category | flops | bytes accessed | tf_op | source)
XLA Modules:
  0.0 62.6 jit_solution(6840800222686243449)
XLA Ops:
  1.9 58.6 %contrastive_square.1 = (f32[192,576]{1,0:T(8,128)}, f32[192,576]{1,0:T(8,128)}) custom-call(bf16[192,1152]{1,0:T(8,128)(2,1)} %pic_hbm.1, bf16[192,576]{1,0:T(8,128)(2,1)} %cap_hbm.1, f32[1152]{0:T(1024)} %gain_hbm.1, bf16[2152,1152]{1,0:T(8,128)(2,1)} %bitcast.5, bf16[2152,1152]{1,0:T(8,128)(2,1)} %exit_hbm.1, bf16[576,1152]{1,0:T(8,128)(2,1)} %map_hbm.1, ...), custom_call_target="tpu_custom_call" | custom-call | tf_op jit(solution)/shard_map/contrastive_square/pallas_call | solution.py:934
  60.5 2.1 %hand_over.1 = (f32[192,576]{1,0:T(8,128)}, f32[192,576]{1,0:T(8,128)}) custom-call(f32[192,576]{1,0:T(8,128)} %get-tuple-element.4.image_hbm, f32[192,576]{1,0:T(8,128)} %get-tuple-element.5.text_hbm), custom_call_target="tpu_custom_call" | custom-call | tf_op jit(solution)/shard_map/hand_over/pallas_call | solution.py:1000

commit v4 on v3

--- a/solution.py
+++ b/solution.py
@@ -572,6 +572,7 @@
     chunk = share // 3 if share % 48 == 0 else share
     chunks = range(share // chunk)
     spans = [slice(first, min(first + TILE, width)) for first in range(0, width, TILE)]
+    x_back = [k % 2 == 0 for k in chunks]
     x_first = [k == 2 for k in chunks]
 
     def block(ref, at):
@@ -764,7 +765,7 @@
 
     d_part[of(2), :] = (d_near[of(3), :] + dot(weights[of(3), late], tbuf[late, :])).astype(BF16)
     through = [
-        push(part(d_part, 2, k), part(d_through, 0, k), by_x if x_first[k] else by_low) for k in chunks
+        push(part(d_part, 2, k), part(d_through, 0, k), by_x if x_back[k] else by_low) for k in chunks
     ]
     d_near[share : 3 * share] += dot(weights[share : 3 * share, late], tbuf[late, :])
     from_x = [None for k in chunks]
@@ -775,7 +776,7 @@
         (from_x, from_low)[at][k] = copy
 
     for k in chunks:
-        at = 0 if x_first[k] else 1
+        at = 0 if x_back[k] else 1
         d_part[lines(at, k)] = d_near[lines(at + 1, k)].astype(BF16)
         send_dir(at, k)
 
@@ -787,7 +788,7 @@
     diagonal_copies = [push(part(y_part, 1, k), part(y_land, 1, k), by_y) for k in chunks]
     y_copies = [push(part(y_part, 0, k), part(y_land, 0, k), by_y) for k in chunks]
     for k in chunks:
-        at = 1 if x_first[k] else 0
+        at = 1 if x_back[k] else 0
         through[k].wait_recv()
         total = d_near[lines(at + 1, k)] + d_through[lines(0, k)].astype(F32)
         d_part[lines(at, k)] = total.astype(BF16)

time: 62.7 us -> 62.4 us (level)
  no operation moved by 1% of the time
where the time goes in v4:
time: 62.4 us; the launch traced here: 62.2 us
  Pallas kernels  60.3 us (97%)
  between operations  1.93 us (3%)
    pallas_call x1, Pallas kernels, square_device(): pl.pallas_call(square_body, out_shape=results, in_specs=[anywhere] * 8, o...  58.2 us
    pallas_call x1, Pallas kernels, square_device(): pl.pallas_call(hand_over, out_shape=results, in_specs=[anywhere, anywhere...  2.07 us

profile of v4, /device:TPU:0, one launch (start us, length us, event | category | flops | bytes accessed | tf_op | source)
XLA Modules:
  0.0 62.2 jit_solution(8813500608722504234)
XLA Ops:
  1.9 58.2 %contrastive_square.1 = (f32[192,576]{1,0:T(8,128)}, f32[192,576]{1,0:T(8,128)}) custom-call(bf16[192,1152]{1,0:T(8,128)(2,1)} %pic_hbm.1, bf16[192,576]{1,0:T(8,128)(2,1)} %cap_hbm.1, f32[1152]{0:T(1024)} %gain_hbm.1, bf16[2152,1152]{1,0:T(8,128)(2,1)} %bitcast.5, bf16[2152,1152]{1,0:T(8,128)(2,1)} %exit_hbm.1, bf16[576,1152]{1,0:T(8,128)(2,1)} %map_hbm.1, ...), custom_call_target="tpu_custom_call" | custom-call | tf_op jit(solution)/shard_map/contrastive_square/pallas_call | solution.py:935
  60.2 2.1 %hand_over.1 = (f32[192,576]{1,0:T(8,128)}, f32[192,576]{1,0:T(8,128)}) custom-call(f32[192,576]{1,0:T(8,128)} %get-tuple-element.4.image_hbm, f32[192,576]{1,0:T(8,128)} %get-tuple-element.5.text_hbm), custom_call_target="tpu_custom_call" | custom-call | tf_op jit(solution)/shard_map/hand_over/pallas_call | solution.py:1001
